TPU v7x, 128 devices: a whole 4x4x4 slice. The times are simulated.
128 devices in a mesh: seq: 32 (over z, x, y_lo), tp: 4 (over y_hi, core).
Axes of the slice: x: 4, y: 4 (y_hi: 2, y_lo: 2; y = y_hi * 2 + y_lo), z: 4, core: 2. Of those that a mesh axis runs over, the one named last changes fastest.
Arguments:
- queries: bfloat16 [8192, 4096], P('seq', 'tp'), may hold values from -48 to 48, as said below
- key_rows: bfloat16 [8192, 512], P('seq', 'tp'), may hold values from -6 to 6, as said below
- value_rows: bfloat16 [8192, 512], P('seq', 'tp'), may hold values from -6 to 6
- projection: bfloat16 [4096, 8192], P('tp'), may hold values from -0.125 to 0.125
Outputs:
- attention_out: bfloat16 [8192, 8192], P('seq', 'tp')
Inputs may be any that keep to these rules, and one draw needn't show every extreme that they name: `queries`: entries of order one; a few queries late in the prompt may align strongly with earlier keys and reach about 45. `key_rows`: entries of order one.
All inputs are finite; a program needn't handle non-finite values.
Results may differ from a plain program's by a relative error of at most 0.012.
Values may be sent and summed in bfloat16 or wider, within the bound.
No kernel may reach another device: no remote copies, remote signals or barrier semaphores. Data moves between devices by JAX's collectives and lax.ppermute only.
A program may use at most 64 MiB of HBM per device.

v0:
```python
import functools

import jax
import jax.numpy as jnp
from jax import lax
from jax.experimental import pallas as pl
from jax.experimental.pallas import tpu as pltpu
from jax.sharding import PartitionSpec as P


NZ, NX, NY, NH, NC = 4, 4, 2, 2, 2
AXES = ("seq", "tp")
HD = 128
UNIT = HD**-0.5 * 1.4426950408889634
LIMIT = 60.0

STEPS = (1, 3, 2)
BLK = 256


def flat(z, x, y, h, c):
    return ((z * NX + x) * NY + y) * NH * NC + h * NC + c


def send(a, move):
    pairs = []
    for z in range(NZ):
        for x in range(NX):
            for y in range(NY):
                for h in range(NH):
                    for c in range(NC):
                        tz, tx, ty, th, tc = move(z, x, y, h, c)
                        tz, tx, ty, th, tc = tz % NZ, tx % NX, ty % NY, th % NH, tc % NC
                        pairs.append((flat(z, x, y, h, c), flat(tz, tx, ty, th, tc)))
    return lax.ppermute(a, AXES, pairs)


def along_x(a, d):
    return send(a, lambda z, x, y, h, c: (z, x + d, y, h, c))


def along_z(a, d):
    return send(a, lambda z, x, y, h, c: (z + d, x, y, h, c))


def exact_fold(h, q_ref, tile, valid, top, acc):
    keys = tile.shape[0]
    q = q_ref[:, pl.ds(pl.multiple_of(h * HD, HD), HD)]
    s = lax.dot_general(q, tile[:, :HD], (((1,), (1,)), ((), ())), preferred_element_type=jnp.float32)
    u = s * UNIT
    if valid is not None:
        u = jnp.where(valid, u, -1e30)
    old = top[h]
    new = jnp.maximum(old, jnp.max(u, axis=1, keepdims=True))
    top[h] = new
    factor = jnp.exp2(old - new)
    p = jnp.exp2(u - jnp.concatenate([new] * (keys // HD), axis=1)).astype(jnp.bfloat16)
    value_mat = jnp.concatenate([tile[:, HD:], jnp.ones((keys, HD), jnp.bfloat16)], axis=1)
    acc[h] = acc[h] * jnp.concatenate([factor, factor], axis=1) + jnp.dot(
        p, value_mat, preferred_element_type=jnp.float32
    )


def fast_fold(q_ref, tile, top, acc, worst):
    keys = tile.shape[0]
    rows = q_ref.shape[0]
    value_mat = jnp.concatenate([tile[:, HD:], jnp.ones((keys, HD), jnp.bfloat16)], axis=1)
    for h in range(acc.shape[0]):
        q = q_ref[:, h * HD : (h + 1) * HD]
        s = lax.dot_general(q, tile[:, :HD], (((1,), (1,)), ((), ())), preferred_element_type=jnp.float32)
        u = s * UNIT - jnp.concatenate([top[h]] * (keys // HD), axis=1)
        high = u[:, :HD]
        for j in range(1, keys // HD):
            high = jnp.maximum(high, u[:, j * HD : (j + 1) * HD])
        p = jnp.exp2(u).astype(jnp.bfloat16)
        acc[h] = acc[h] + jnp.dot(p, value_mat, preferred_element_type=jnp.float32)
        worst = jnp.maximum(worst, jnp.max(high.reshape(rows // 8, 8, HD), axis=0))
    return worst


def fold_own(q_ref, own, y, top, acc):
    rows = q_ref.shape[0]
    top[...] = jnp.full(top.shape, -1e30, jnp.float32)
    acc[...] = jnp.zeros(acc.shape, jnp.float32)
    r = lax.broadcasted_iota(jnp.int32, (rows, 2 * BLK), 0)
    k = lax.broadcasted_iota(jnp.int32, (rows, 2 * BLK), 1)
    position = lax.div(k, 256) * 128 + lax.rem(k, 128)
    position = position + jnp.where(lax.rem(lax.div(k, 128), 2) == 0, 0, jnp.where(y == 0, 256, -256))
    valid = position <= r

    def head(h, carry):
        exact_fold(h, q_ref, own[...], valid, top, acc)
        return carry

    lax.fori_loop(0, acc.shape[0], head, 0, unroll=4)


def own_kernel(place, q_ref, own, top, acc):
    fold_own(q_ref, own, place[2], top, acc)


def step_kernel(place, q_ref, top_in, acc_in, *rest, last, blocks):
    n = len(blocks)
    refs, rest = rest[:n], rest[n:]
    if last:
        w_ref, heads_ref, x_ref, held, top, acc, w_buf, sems = rest
        copies = load_columns(w_ref, place[3], w_buf, sems)
    else:
        top, acc, held = rest
    z, x = place[0], place[1]
    count = jnp.int32(0)
    for ref, sources in zip(refs, blocks):
        for i, (dx, dz) in enumerate(sources):
            needed = lax.rem(z + dz, NZ) * NX + lax.rem(x + dx, NX) < z * NX + x

            @pl.when(needed)
            def _(ref=ref, i=i, at=count):
                held[pl.ds(pl.multiple_of(at * BLK, BLK), BLK), :] = ref[i * BLK : (i + 1) * BLK, :]

            count = count + needed.astype(jnp.int32)

    top[...] = top_in[...]
    acc[...] = acc_in[...]

    def keys_at(i, n):
        return held[pl.ds(pl.multiple_of(i * n, n), n), :]

    def odd(w):
        return fast_fold(q_ref, keys_at(count - 1, BLK), top, acc, w)

    worst = lax.fori_loop(
        0,
        lax.div(count, 2),
        lambda i, w: fast_fold(q_ref, keys_at(i, 2 * BLK), top, acc, w),
        jnp.full((8, HD), -1e30, jnp.float32),
    )
    worst = lax.cond(lax.rem(count, 2) == 1, odd, lambda w: w, worst)

    @pl.when(jnp.max(worst) > LIMIT)
    def _():
        acc[...] = acc_in[...]

        def again(i, carry):
            def head(h, c):
                exact_fold(h, q_ref, keys_at(i, BLK), None, top, acc)
                return c

            return lax.fori_loop(0, acc.shape[0], head, carry)

        lax.fori_loop(0, count, again, 0)

    if last:
        for h in range(acc.shape[0]):
            a = acc[h]
            heads_ref[:, h * HD : (h + 1) * HD] = (a[:, :HD] / a[:, HD:]).astype(jnp.bfloat16)
        multiply_columns(heads_ref, w_buf, copies, x_ref)


WIDTH, CHUNK = 2048, 512


def load_columns(w_ref, part, w_buf, sems):
    copies = []
    for j in range(WIDTH // CHUNK):
        at = pl.multiple_of(part * WIDTH + j * CHUNK, CHUNK)
        copies.append(
            pltpu.make_async_copy(w_ref.at[:, pl.ds(at, CHUNK)], w_buf.at[:, pl.ds(j * CHUNK, CHUNK)], sems.at[j])
        )
        copies[-1].start()
    return copies


def multiply_columns(heads_ref, w_buf, copies, out_ref):
    for j, copy in enumerate(copies):
        copy.wait()
        out_ref[:, j * CHUNK : (j + 1) * CHUNK] = jnp.dot(
            heads_ref[...], w_buf[:, j * CHUNK : (j + 1) * CHUNK], preferred_element_type=jnp.float32
        ).astype(out_ref.dtype)


def project_kernel(part, heads_ref, w_ref, out_ref, w_buf, sems):
    multiply_columns(heads_ref, w_buf, load_columns(w_ref, part[0], w_buf, sems), out_ref)


SMEM = pl.BlockSpec(memory_space=pltpu.SMEM)
VMEM = pl.BlockSpec(memory_space=pltpu.VMEM)
HBM = pl.BlockSpec(memory_space=pltpu.HBM)
W_SCRATCH = [pltpu.VMEM((1024, WIDTH), jnp.bfloat16), pltpu.SemaphoreType.DMA((WIDTH // CHUNK,))]


def cost(blocks, mib):
    n = blocks * 512 * 2048
    return pl.CostEstimate(flops=4 * n * HD, bytes_accessed=mib << 20, transcendentals=n)


def state_of(rows, heads):
    return (
        jax.ShapeDtypeStruct((heads, rows, HD), jnp.float32),
        jax.ShapeDtypeStruct((heads, rows, 2 * HD), jnp.float32),
    )


def attend(place, queries, state, own, operands, projection=None):
    arrays, blocks = [a for a, _ in operands], [b for _, b in operands]
    rows, width = queries.shape
    first, last = own is not None, projection is not None
    shapes = state_of(rows, width // HD)
    in_state = [own] if first else list(state)
    held = [] if first else [pltpu.VMEM((sum(len(b) for b in blocks) * BLK, 2 * HD), jnp.bfloat16)]
    buffers = [pltpu.VMEM(s.shape, s.dtype) for s in shapes]
    out = (jax.ShapeDtypeStruct((rows, width), jnp.bfloat16), jax.ShapeDtypeStruct((rows, WIDTH), jnp.bfloat16))
    return pl.pallas_call(
        own_kernel if first else functools.partial(step_kernel, last=last, blocks=blocks),
        out_shape=out if last else shapes,
        in_specs=[SMEM, VMEM] + [VMEM] * (len(in_state) + len(arrays)) + [HBM] * last,
        out_specs=(VMEM, VMEM),
        scratch_shapes=held + (buffers + W_SCRATCH if last else []),
        compiler_params=pltpu.CompilerParams(vmem_limit_bytes=(45 if last else 20) << 20),
        cost_estimate=cost(1 if first else 4, 8),
        name="attend_last" if last else "attend_own" if first else "attend_step",
    )(place, queries, *in_state, *arrays, *([projection] if last else []))


def pack_kernel(k_ref, v_ref, out_ref):
    out_ref[:, :HD] = k_ref[...]
    out_ref[:, HD:] = v_ref[...]


def pack(key_rows, value_rows):
    return pl.pallas_call(
        pack_kernel,
        out_shape=jax.ShapeDtypeStruct((key_rows.shape[0], 2 * HD), jnp.bfloat16),
        in_specs=[VMEM, VMEM],
        out_specs=VMEM,
        compiler_params=pltpu.CompilerParams(vmem_limit_bytes=4 << 20),
        name="pack",
    )(key_rows, value_rows)


def project(heads_out, projection, part):
    rows = heads_out.shape[0]
    return pl.pallas_call(
        project_kernel,
        out_shape=jax.ShapeDtypeStruct((rows, WIDTH), jnp.bfloat16),
        in_specs=[SMEM, VMEM, HBM],
        out_specs=VMEM,
        scratch_shapes=W_SCRATCH,
        compiler_params=pltpu.CompilerParams(vmem_limit_bytes=50 << 20),
        cost_estimate=pl.CostEstimate(flops=2 * rows * 1024 * WIDTH, bytes_accessed=6 << 20, transcendentals=0),
        name="project",
    )(part.reshape(1), heads_out, projection)


def add(a, b):
    return (a.astype(jnp.float32) + b.astype(jnp.float32)).astype(jnp.bfloat16)


def on_device(queries, key_rows, value_rows, projection):
    seq = lax.axis_index("seq").astype(jnp.int32)
    tp = lax.axis_index("tp").astype(jnp.int32)
    place = jnp.stack([seq // (NX * NY), (seq // NY) % NX, seq % NY, tp ^ 3])

    both = pack(key_rows, value_rows)
    near = send(both, lambda z, x, y, h, c: (z, x, y + 1, h, c))
    pair_a = jnp.concatenate([both[:128], near[:128]], axis=0)
    pair_b = jnp.concatenate([both[128:], near[128:]], axis=0)
    own = jnp.concatenate([pair_a, pair_b], axis=0)
    ax = [along_x(pair_a, d) for d in STEPS]
    bz = [along_z(pair_b, d) for d in STEPS]
    state = attend(place, queries, None, own, [])
    ax, bz, state = lax.optimization_barrier((ax, bz, state))
    all_a = jnp.concatenate([pair_a] + ax, axis=0)
    all_b = jnp.concatenate([pair_b] + bz, axis=0)

    def a_runs(d):
        return [((4 - e) % 4, 4 - d) for e in (0,) + STEPS]

    def b_runs(d):
        return [(4 - d, (4 - e) % 4) for e in (0,) + STEPS]

    az = [along_z(all_a, d) for d in STEPS[:2]]
    bx = [along_x(all_b, d) for d in STEPS[:2]]
    early = [(a, [(4 - d, 0)]) for a, d in zip(ax, STEPS)] + [(b, [(0, 4 - d)]) for b, d in zip(bz, STEPS)]
    state = attend(place, queries, state, None, early)
    az, bx, all_a, all_b, state = lax.optimization_barrier((az, bx, all_a, all_b, state))
    az.append(along_z(all_a, STEPS[2]))
    bx.append(along_x(all_b, STEPS[2]))
    state = attend(place, queries, state, None, [(az[i], a_runs(STEPS[i])) for i in (0, 1)])
    state = attend(place, queries, state, None, [(bx[i], b_runs(STEPS[i])) for i in (0, 1)])
    rest = [(az[2], a_runs(STEPS[2])), (bx[2], b_runs(STEPS[2]))]
    heads_out, far = attend(place, queries, state, None, rest, projection)

    far = send(far, lambda z, x, y, h, c: (z, x, y, h, c + 1))
    cross = add(project(heads_out, projection, tp ^ 2), far)
    heads_out, cross = lax.optimization_barrier((heads_out, cross))
    cross = send(cross, lambda z, x, y, h, c: (z, x, y, h + 1, c))
    side = project(heads_out, projection, tp ^ 1)
    side = send(side, lambda z, x, y, h, c: (z, x, y, h, c + 1))
    mine = project(heads_out, projection, tp)
    total = mine.astype(jnp.float32) + side.astype(jnp.float32) + cross.astype(jnp.float32)
    return total.astype(jnp.bfloat16)


def solution(mesh):
    in_specs = (P("seq", "tp"), P("seq", "tp"), P("seq", "tp"), P("tp", None))
    return jax.shard_map(on_device, mesh=mesh, in_specs=in_specs, out_specs=P("seq", "tp"), check_vma=False)
```

profile of v0, /device:TPU:126, one launch (start us, length us, event | category | flops | bytes accessed | tf_op | source)
XLA Modules:
  0.0 162.8 jit_solution(12619193136922138036)
XLA Ops:
  0.0 0.9 copy-done.1
  0.9 0.8 copy-done.2
  1.8 0.8 collective-permute-start
  2.6 4.5 %collective-permute-done = bf16[256,256]{1,0:T(8,128)(2,1)S(1)} collective-permute-done((bf16[256,256]{1,0:T(8,128)(2,1)S(1)}, bf16[256,256]{1,0:T(8,128)(2,1)S(1)}, u32[]{:S(2)}, u32[]{:S(2)}) %collective-permute-start) | collective-permute-done | bytes 131104 | tf_op jit(solution)/shard_map/ppermute | solution.py:35
  7.3 2.0 %collective-permute-start.5 = (bf16[256,256]{1,0:T(8,128)(2,1)S(1)}, bf16[256,256]{1,0:T(8,128)(2,1)S(1)}, u32[]{:S(2)}, u32[]{:S(2)}) collective-permute-start(bf16[256,256]{1,0:T(8,128)(2,1)S(1)} %pad_maximum_fusion.2), channel_id=1, source_target_pairs={{0,96},{1,97},{2,98},{3,99},{4,100},{5,101},{6,102},{7,103},{8,104... | collective-permute-start | bytes 393224 | tf_op jit(solution)/shard_map/ppermute | solution.py:35
  10.4 1.5 collective-permute-start.2
  12.0 1.5 collective-permute-done.4.rest_3_
  13.5 1.4 collective-permute-start.3
  14.9 3.1 %attend_own.1 = (f32[8,256,128]{2,1,0:T(8,128)S(1)}, f32[8,256,256]{2,1,0:T(8,128)S(1)}) custom-call(s32[4]{0:T(128)S(1)} %pad_add_fusion.place, bf16[256,1024]{1,0:T(8,128)(2,1)S(1)} %copy-done, bf16[512,256]{1,0:T(8,128)(2,1)S(1)} %pad_maximum_fusion.own), custom_call_target="tpu_custom_call" | custom-call | flops 536870912 | bytes 8388608 | tf_op jit(solution)/shard_map/attend_own/pallas_call | solution.py:212
  18.1 2.0 %collective-permute-done.3.rest_2_ = bf16[256,256]{1,0:T(8,128)(2,1)S(1)} collective-permute-done((bf16[256,256]{1,0:T(8,128)(2,1)S(1)}, bf16[256,256]{1,0:T(8,128)(2,1)S(1)}, u32[]{:S(2)}, u32[]{:S(2)}) %collective-permute-start.3) | collective-permute-done | bytes 131104 | tf_op jit(solution)/shard_map/ppermute | solution.py:35
  20.1 0.9 collective-permute-start.10
  21.0 2.4 %collective-permute-start.9 = (bf16[1024,256]{1,0:T(8,128)(2,1)S(1)}, bf16[1024,256]{1,0:T(8,128)(2,1)S(1)}, u32[]{:S(2)}, u32[]{:S(2)}) collective-permute-start(bf16[1024,256]{1,0:T(8,128)(2,1)S(1)} %constant_dynamic-update-slice_fusion.5), channel_id=1, source_target_pairs={{0,8},{1,9},{2,10},{3,11},{4,12},{5,13},{6,14},{7,15},{8,16},{9,17... | collective-permute-start | bytes 1572872 | tf_op jit(solution)/shard_map/ppermute | solution.py:35
  23.5 1.0 collective-permute-start.7
  24.4 1.1 collective-permute-start.8
  25.6 25.7 %attend_step.3 = (f32[8,256,128]{2,1,0:T(8,128)S(1)}, f32[8,256,256]{2,1,0:T(8,128)S(1)}) custom-call(s32[4]{0:T(128)S(1)} %pad_add_fusion.place, bf16[256,1024]{1,0:T(8,128)(2,1)S(1)} %copy-done, f32[8,256,128]{2,1,0:T(8,128)S(1)} %get-tuple-element.41.top_in, f32[8,256,256]{2,1,0:T(8,128)S(1)} %get-tuple-element.42.acc_in, ...), custom_call_target="tpu_custom_call" | custom-call | flops 2147483648 | bytes 8388608 | tf_op jit(solution)/shard_map/attend_step/pallas_call | solution.py:212
  51.5 6.5 %attend_step.4 = (f32[8,256,128]{2,1,0:T(8,128)S(1)}, f32[8,256,256]{2,1,0:T(8,128)S(1)}) custom-call(s32[4]{0:T(128)S(1)} %pad_add_fusion.place, bf16[256,1024]{1,0:T(8,128)(2,1)S(1)} %copy-done, f32[8,256,128]{2,1,0:T(8,128)S(1)} %get-tuple-element.45.top_in, f32[8,256,256]{2,1,0:T(8,128)S(1)} %get-tuple-element.46.acc_in, ...), custom_call_target="tpu_custom_call" | custom-call | flops 2147483648 | bytes 8388608 | tf_op jit(solution)/shard_map/attend_step/pallas_call | solution.py:212
  58.0 33.9 %attend_step.5 = (f32[8,256,128]{2,1,0:T(8,128)S(1)}, f32[8,256,256]{2,1,0:T(8,128)S(1)}) custom-call(s32[4]{0:T(128)S(1)} %pad_add_fusion.place, bf16[256,1024]{1,0:T(8,128)(2,1)S(1)} %copy-done, f32[8,256,128]{2,1,0:T(8,128)S(1)} %get-tuple-element.49.top_in, f32[8,256,256]{2,1,0:T(8,128)S(1)} %get-tuple-element.50.acc_in, ...), custom_call_target="tpu_custom_call" | custom-call | flops 2147483648 | bytes 8388608 | tf_op jit(solution)/shard_map/attend_step/pallas_call | solution.py:212
  91.9 35.6 %attend_last.1 = (bf16[256,1024]{1,0:T(8,128)(2,1)S(1)}, bf16[256,2048]{1,0:T(8,128)(2,1)S(1)}) custom-call(s32[4]{0:T(128)S(1)} %pad_add_fusion.place, bf16[256,1024]{1,0:T(8,128)(2,1)S(1)} %copy-done, f32[8,256,128]{2,1,0:T(8,128)S(1)} %get-tuple-element.53.top_in, f32[8,256,256]{2,1,0:T(8,128)S(1)} %get-tuple-element.54.acc_in, ...), custom_call_target="tpu_custom_call" | custom-call | flops 2147483648 | bytes 8388608 | tf_op jit(solution)/shard_map/attend_last/pallas_call | solution.py:212
  127.6 3.0 %project.3 = bf16[256,2048]{1,0:T(8,128)(2,1)S(1)} custom-call(s32[1]{0:T(128)} %bitcast.5.part, bf16[256,1024]{1,0:T(8,128)(2,1)S(1)} %get-tuple-element.59.heads_ref, bf16[1024,8192]{1,0:T(8,128)(2,1)} %w_ref.5), custom_call_target="tpu_custom_call" | custom-call | flops 1073741824 | bytes 6291456 | tf_op jit(solution)/shard_map/project/pallas_call | solution.py:242
  131.0 3.0 %project.5 = bf16[256,2048]{1,0:T(8,128)(2,1)S(1)} custom-call(s32[1]{0:T(128)} %bitcast.6.part, bf16[256,1024]{1,0:T(8,128)(2,1)S(1)} %get-tuple-element.59.heads_ref, bf16[1024,8192]{1,0:T(8,128)(2,1)} %w_ref.5), custom_call_target="tpu_custom_call" | custom-call | flops 1073741824 | bytes 6291456 | tf_op jit(solution)/shard_map/project/pallas_call | solution.py:242
  134.6 1.2 collective-permute-start.15
  135.8 3.0 %project.4 = bf16[256,2048]{1,0:T(8,128)(2,1)S(1)} custom-call(s32[1]{0:T(128)} %bitcast.part, bf16[256,1024]{1,0:T(8,128)(2,1)S(1)} %get-tuple-element.59.heads_ref, bf16[1024,8192]{1,0:T(8,128)(2,1)} %w_ref.5), custom_call_target="tpu_custom_call" | custom-call | flops 1073741824 | bytes 6291456 | tf_op jit(solution)/shard_map/project/pallas_call | solution.py:242
  138.9 22.4 %collective-permute-done.15 = bf16[256,2048]{1,0:T(8,128)(2,1)S(1)} collective-permute-done((bf16[256,2048]{1,0:T(8,128)(2,1)S(1)}, bf16[256,2048]{1,0:T(8,128)(2,1)S(1)}, u32[]{:S(2)}, u32[]{:S(2)}) %collective-permute-start.15) | collective-permute-done | bytes 1048608 | tf_op jit(solution)/shard_map/ppermute | solution.py:35
  161.3 1.5 add_convert_fusion
  (36 shorter events, 2.7 us)
Async XLA Ops:
  0.0 14.9 %copy-start = (bf16[256,1024]{1,0:T(8,128)(2,1)S(1)}, bf16[256,1024]{1,0:T(8,128)(2,1)}, u32[]{:S(2)}) copy-start(bf16[256,1024]{1,0:T(8,128)(2,1)} %q_ref.9) | copy-start | bytes 1572868
  0.0 0.9 copy-start.1
  0.9 0.8 copy-start.2
  1.8 5.3 %collective-permute-start = (bf16[256,256]{1,0:T(8,128)(2,1)S(1)}, bf16[256,256]{1,0:T(8,128)(2,1)S(1)}, u32[]{:S(2)}, u32[]{:S(2)}) collective-permute-start(bf16[256,256]{1,0:T(8,128)(2,1)S(1)} %pack.1), channel_id=1, source_target_pairs={{0,4},{1,5},{2,6},{3,7},{4,0},{5,1},{6,2},{7,3},{8,12},{9,13},{10,... | collective-permute-start | bytes 393224 | tf_op jit(solution)/shard_map/ppermute | solution.py:35
  7.1 6.3 %collective-permute-start.4 = (bf16[256,256]{1,0:T(8,128)(2,1)S(1)}, bf16[256,256]{1,0:T(8,128)(2,1)S(1)}, u32[]{:S(2)}, u32[]{:S(2)}) collective-permute-start(bf16[256,256]{1,0:T(8,128)(2,1)S(1)} %pad_maximum_fusion.2), channel_id=1, source_target_pairs={{0,32},{1,33},{2,34},{3,35},{4,36},{5,37},{6,38},{7,39},{8,40},{9,... | collective-permute-start | bytes 393224 | tf_op jit(solution)/shard_map/ppermute | solution.py:35
  7.3 10.8 %collective-permute-start.5 = (bf16[256,256]{1,0:T(8,128)(2,1)S(1)}, bf16[256,256]{1,0:T(8,128)(2,1)S(1)}, u32[]{:S(2)}, u32[]{:S(2)}) collective-permute-start(bf16[256,256]{1,0:T(8,128)(2,1)S(1)} %pad_maximum_fusion.2), channel_id=1, source_target_pairs={{0,96},{1,97},{2,98},{3,99},{4,100},{5,101},{6,102},{7,103},{8,104... | collective-permute-start | bytes 393224 | tf_op jit(solution)/shard_map/ppermute | solution.py:35
  9.3 8.8 %collective-permute-start.6 = (bf16[256,256]{1,0:T(8,128)(2,1)S(1)}, bf16[256,256]{1,0:T(8,128)(2,1)S(1)}, u32[]{:S(2)}, u32[]{:S(2)}) collective-permute-start(bf16[256,256]{1,0:T(8,128)(2,1)S(1)} %pad_maximum_fusion.2), channel_id=1, source_target_pairs={{0,64},{1,65},{2,66},{3,67},{4,68},{5,69},{6,70},{7,71},{8,72},{9,... | collective-permute-start | bytes 393224 | tf_op jit(solution)/shard_map/ppermute | solution.py:35
  9.9 8.2 %collective-permute-start.1 = (bf16[256,256]{1,0:T(8,128)(2,1)S(1)}, bf16[256,256]{1,0:T(8,128)(2,1)S(1)}, u32[]{:S(2)}, u32[]{:S(2)}) collective-permute-start(bf16[256,256]{1,0:T(8,128)(2,1)S(1)} %pad_maximum_fusion.1), channel_id=1, source_target_pairs={{0,8},{1,9},{2,10},{3,11},{4,12},{5,13},{6,14},{7,15},{8,16},{9,17... | collective-permute-start | bytes 393224 | tf_op jit(solution)/shard_map/ppermute | solution.py:35
  10.4 7.7 %collective-permute-start.2 = (bf16[256,256]{1,0:T(8,128)(2,1)S(1)}, bf16[256,256]{1,0:T(8,128)(2,1)S(1)}, u32[]{:S(2)}, u32[]{:S(2)}) collective-permute-start(bf16[256,256]{1,0:T(8,128)(2,1)S(1)} %pad_maximum_fusion.1), channel_id=1, source_target_pairs={{0,24},{1,25},{2,26},{3,27},{4,28},{5,29},{6,30},{7,31},{8,0},{9,1... | collective-permute-start | bytes 393224 | tf_op jit(solution)/shard_map/ppermute | solution.py:35
  13.5 6.6 %collective-permute-start.3 = (bf16[256,256]{1,0:T(8,128)(2,1)S(1)}, bf16[256,256]{1,0:T(8,128)(2,1)S(1)}, u32[]{:S(2)}, u32[]{:S(2)}) collective-permute-start(bf16[256,256]{1,0:T(8,128)(2,1)S(1)} %pad_maximum_fusion.1), channel_id=1, source_target_pairs={{0,16},{1,17},{2,18},{3,19},{4,20},{5,21},{6,22},{7,23},{8,24},{9,... | collective-permute-start | bytes 393224 | tf_op jit(solution)/shard_map/ppermute | solution.py:35
  20.1 31.1 %collective-permute-start.10 = (bf16[1024,256]{1,0:T(8,128)(2,1)S(1)}, bf16[1024,256]{1,0:T(8,128)(2,1)S(1)}, u32[]{:S(2)}, u32[]{:S(2)}) collective-permute-start(bf16[1024,256]{1,0:T(8,128)(2,1)S(1)} %constant_dynamic-update-slice_fusion.5), channel_id=1, source_target_pairs={{0,24},{1,25},{2,26},{3,27},{4,28},{5,29},{6,30},{7,31},{8,0},{9,1... | collective-permute-start | bytes 1572872 | tf_op jit(solution)/shard_map/ppermute | solution.py:35
  21.0 30.3 %collective-permute-start.9 = (bf16[1024,256]{1,0:T(8,128)(2,1)S(1)}, bf16[1024,256]{1,0:T(8,128)(2,1)S(1)}, u32[]{:S(2)}, u32[]{:S(2)}) collective-permute-start(bf16[1024,256]{1,0:T(8,128)(2,1)S(1)} %constant_dynamic-update-slice_fusion.5), channel_id=1, source_target_pairs={{0,8},{1,9},{2,10},{3,11},{4,12},{5,13},{6,14},{7,15},{8,16},{9,17... | collective-permute-start | bytes 1572872 | tf_op jit(solution)/shard_map/ppermute | solution.py:35
  23.5 27.8 %collective-permute-start.7 = (bf16[1024,256]{1,0:T(8,128)(2,1)S(1)}, bf16[1024,256]{1,0:T(8,128)(2,1)S(1)}, u32[]{:S(2)}, u32[]{:S(2)}) collective-permute-start(bf16[1024,256]{1,0:T(8,128)(2,1)S(1)} %constant_dynamic-update-slice_fusion), channel_id=1, source_target_pairs={{0,32},{1,33},{2,34},{3,35},{4,36},{5,37},{6,38},{7,39},{8,40},{9,... | collective-permute-start | bytes 1572872 | tf_op jit(solution)/shard_map/ppermute | solution.py:35
  24.4 26.8 %collective-permute-start.8 = (bf16[1024,256]{1,0:T(8,128)(2,1)S(1)}, bf16[1024,256]{1,0:T(8,128)(2,1)S(1)}, u32[]{:S(2)}, u32[]{:S(2)}) collective-permute-start(bf16[1024,256]{1,0:T(8,128)(2,1)S(1)} %constant_dynamic-update-slice_fusion), channel_id=1, source_target_pairs={{0,96},{1,97},{2,98},{3,99},{4,100},{5,101},{6,102},{7,103},{8,104... | collective-permute-start | bytes 1572872 | tf_op jit(solution)/shard_map/ppermute | solution.py:35
  51.3 40.6 %collective-permute-start.11 = (bf16[1024,256]{1,0:T(8,128)(2,1)S(1)}, bf16[1024,256]{1,0:T(8,128)(2,1)S(1)}, u32[]{:S(2)}, u32[]{:S(2)}) collective-permute-start(bf16[1024,256]{1,0:T(8,128)(2,1)S(1)} %constant_dynamic-update-slice_fusion), channel_id=1, source_target_pairs={{0,64},{1,65},{2,66},{3,67},{4,68},{5,69},{6,70},{7,71},{8,72},{9,... | collective-permute-start | bytes 1572872 | tf_op jit(solution)/shard_map/ppermute | solution.py:35
  51.4 40.5 %collective-permute-start.12 = (bf16[1024,256]{1,0:T(8,128)(2,1)S(1)}, bf16[1024,256]{1,0:T(8,128)(2,1)S(1)}, u32[]{:S(2)}, u32[]{:S(2)}) collective-permute-start(bf16[1024,256]{1,0:T(8,128)(2,1)S(1)} %constant_dynamic-update-slice_fusion.5), channel_id=1, source_target_pairs={{0,16},{1,17},{2,18},{3,19},{4,20},{5,21},{6,22},{7,23},{8,24},{9,... | collective-permute-start | bytes 1572872 | tf_op jit(solution)/shard_map/ppermute | solution.py:35
  127.5 3.1 %collective-permute-start.13 = (bf16[256,2048]{1,0:T(8,128)(2,1)S(1)}, bf16[256,2048]{1,0:T(8,128)(2,1)S(1)}, u32[]{:S(2)}, u32[]{:S(2)}) collective-permute-start(bf16[256,2048]{1,0:T(8,128)(2,1)S(1)} %get-tuple-element.58), channel_id=1, source_target_pairs={{0,1},{1,0},{2,3},{3,2},{4,5},{5,4},{6,7},{7,6},{8,9},{9,8},{10,11... | collective-permute-start | bytes 3145736 | tf_op jit(solution)/shard_map/ppermute | solution.py:35
  134.0 4.8 %collective-permute-start.14 = (bf16[256,2048]{1,0:T(8,128)(2,1)S(1)}, bf16[256,2048]{1,0:T(8,128)(2,1)S(1)}, u32[]{:S(2)}, u32[]{:S(2)}) collective-permute-start(bf16[256,2048]{1,0:T(8,128)(2,1)S(1)} %project.5), channel_id=1, source_target_pairs={{0,1},{1,0},{2,3},{3,2},{4,5},{5,4},{6,7},{7,6},{8,9},{9,8},{10,11... | collective-permute-start | bytes 3145736 | tf_op jit(solution)/shard_map/ppermute | solution.py:35
  134.6 26.7 %collective-permute-start.15 = (bf16[256,2048]{1,0:T(8,128)(2,1)S(1)}, bf16[256,2048]{1,0:T(8,128)(2,1)S(1)}, u32[]{:S(2)}, u32[]{:S(2)}) collective-permute-start(bf16[256,2048]{1,0:T(8,128)(2,1)S(1)} %add_convert_fusion.1), channel_id=1, source_target_pairs={{0,2},{1,3},{2,0},{3,1},{4,6},{5,7},{6,4},{7,5},{8,10},{9,11},{10,... | collective-permute-start | bytes 3145736 | tf_op jit(solution)/shard_map/ppermute | solution.py:35
where the time goes:
time: 163 us
  Pallas kernels  114 us (70%)
  waiting for transfers between devices  30.4 us (19%)
  starting transfers between devices  14.4 us (9%)
  other arithmetic  2.01 us (1%)
  local copies, waits for them, and re-layouts  1.84 us (1%)
    pallas_call x5, Pallas kernels, attend(): pl.pallas_call(own_kernel if first else functools.partial(step_kernel, la...  105 us
    ppermute x16, waiting for transfers between devices, send(): return lax.ppermute(a, AXES, pairs)  30.4 us
    ppermute x16, starting transfers between devices, send(): return lax.ppermute(a, AXES, pairs)  14.4 us
    pallas_call x3, Pallas kernels, project(): pl.pallas_call(project_kernel, out_shape=jax.ShapeDtypeStruct((rows, WIDT...  9.08 us
  transfers between devices with their start and end apart: 16, of which 4 were waited for; matrix products, arithmetic and copies ran while one was open for 0% of the time, Pallas kernels for 46%

commit v1 on v0

--- a/solution.py
+++ b/solution.py
@@ -35,12 +35,11 @@
     return lax.ppermute(a, AXES, pairs)
 
 
-def along_x(a, d):
-    return send(a, lambda z, x, y, h, c: (z, x + d, y, h, c))
-
-
-def along_z(a, d):
-    return send(a, lambda z, x, y, h, c: (z + d, x, y, h, c))
+def along(a, d, second):
+    def move(z, x, y, h, c):
+        return (z, x + d, y, h, c) if (c == 0) != second else (z + d, x, y, h, c)
+
+    return send(a, move)
 
 
 def exact_fold(h, q_ref, tile, valid, top, acc):
@@ -110,7 +109,8 @@
     z, x = place[0], place[1]
     count = jnp.int32(0)
     for ref, sources in zip(refs, blocks):
-        for i, (dx, dz) in enumerate(sources):
+        for i, (du, dv) in enumerate(sources):
+            dx, dz = jnp.where(place[4] == 0, du, dv), jnp.where(place[4] == 0, dv, du)
             needed = lax.rem(z + dz, NZ) * NX + lax.rem(x + dx, NX) < z * NX + x
 
             @pl.when(needed)
@@ -258,36 +258,34 @@
 def on_device(queries, key_rows, value_rows, projection):
     seq = lax.axis_index("seq").astype(jnp.int32)
     tp = lax.axis_index("tp").astype(jnp.int32)
-    place = jnp.stack([seq // (NX * NY), (seq // NY) % NX, seq % NY, tp ^ 3])
+    place = jnp.stack([seq // (NX * NY), (seq // NY) % NX, seq % NY, tp ^ 3, tp % NC])
 
     both = pack(key_rows, value_rows)
     near = send(both, lambda z, x, y, h, c: (z, x, y + 1, h, c))
     pair_a = jnp.concatenate([both[:128], near[:128]], axis=0)
     pair_b = jnp.concatenate([both[128:], near[128:]], axis=0)
     own = jnp.concatenate([pair_a, pair_b], axis=0)
-    ax = [along_x(pair_a, d) for d in STEPS]
-    bz = [along_z(pair_b, d) for d in STEPS]
+    first_a = [along(pair_a, d, False) for d in STEPS]
+    first_b = [along(pair_b, d, True) for d in STEPS]
     state = attend(place, queries, None, own, [])
-    ax, bz, state = lax.optimization_barrier((ax, bz, state))
-    all_a = jnp.concatenate([pair_a] + ax, axis=0)
-    all_b = jnp.concatenate([pair_b] + bz, axis=0)
-
-    def a_runs(d):
-        return [((4 - e) % 4, 4 - d) for e in (0,) + STEPS]
-
-    def b_runs(d):
-        return [(4 - d, (4 - e) % 4) for e in (0,) + STEPS]
-
-    az = [along_z(all_a, d) for d in STEPS[:2]]
-    bx = [along_x(all_b, d) for d in STEPS[:2]]
-    early = [(a, [(4 - d, 0)]) for a, d in zip(ax, STEPS)] + [(b, [(0, 4 - d)]) for b, d in zip(bz, STEPS)]
+    first_a, first_b, state = lax.optimization_barrier((first_a, first_b, state))
+    all_a = jnp.concatenate([pair_a] + first_a, axis=0)
+    all_b = jnp.concatenate([pair_b] + first_b, axis=0)
+
+    def runs(d, a):
+        return [((4 - e) % 4, 4 - d) if a else (4 - d, (4 - e) % 4) for e in (0,) + STEPS]
+
+    near_a = [(along(all_a, d, True), runs(d, True)) for d in STEPS[:2]]
+    near_b = [(along(all_b, d, False), runs(d, False)) for d in STEPS[:2]]
+    early = [(a, [(4 - d, 0)]) for a, d in zip(first_a, STEPS)] + [(b, [(0, 4 - d)]) for b, d in zip(first_b, STEPS)]
     state = attend(place, queries, state, None, early)
-    az, bx, all_a, all_b, state = lax.optimization_barrier((az, bx, all_a, all_b, state))
-    az.append(along_z(all_a, STEPS[2]))
-    bx.append(along_x(all_b, STEPS[2]))
-    state = attend(place, queries, state, None, [(az[i], a_runs(STEPS[i])) for i in (0, 1)])
-    state = attend(place, queries, state, None, [(bx[i], b_runs(STEPS[i])) for i in (0, 1)])
-    rest = [(az[2], a_runs(STEPS[2])), (bx[2], b_runs(STEPS[2]))]
+    arrays, all_a, state = lax.optimization_barrier(([a for a, _ in near_a], all_a, state))
+    far_a = along(all_a, STEPS[2], True)
+    state = attend(place, queries, state, None, [(a, r) for a, (_, r) in zip(arrays, near_a)])
+    arrays, all_b, state = lax.optimization_barrier(([b for b, _ in near_b], all_b, state))
+    far_b = along(all_b, STEPS[2], False)
+    state = attend(place, queries, state, None, [(b, r) for b, (_, r) in zip(arrays, near_b)])
+    rest = [(far_a, runs(STEPS[2], True)), (far_b, runs(STEPS[2], False))]
     heads_out, far = attend(place, queries, state, None, rest, projection)
 
     far = send(far, lambda z, x, y, h, c: (z, x, y, h, c + 1))

time: 163 us -> 168 us (1.031)
  the two profiles are of different devices: /device:TPU:126 before, /device:TPU:110 now
where the time goes in v1:
time: 168 us; the launch traced here: 167 us
  Pallas kernels  114 us (68%)
  waiting for transfers between devices  27.6 us (16%)
  starting transfers between devices  21.8 us (13%)
  other arithmetic  1.93 us (1%)
  local copies, waits for them, and re-layouts  1.92 us (1%)
    pallas_call x5, Pallas kernels, attend(): pl.pallas_call(own_kernel if first else functools.partial(step_kernel, la...  105 us
    ppermute x16, waiting for transfers between devices, send(): return lax.ppermute(a, AXES, pairs)  27.6 us
    ppermute x16, starting transfers between devices, send(): return lax.ppermute(a, AXES, pairs)  21.8 us
    pallas_call x3, Pallas kernels, project(): pl.pallas_call(project_kernel, out_shape=jax.ShapeDtypeStruct((rows, WIDT...  9.08 us
  transfers between devices with their start and end apart: 16, of which 3 were waited for; matrix products, arithmetic and copies ran while one was open for 0% of the time, Pallas kernels for 45%

profile of v1, /device:TPU:110, one launch (start us, length us, event | category | flops | bytes accessed | tf_op | source)
XLA Modules:
  0.0 167.5 jit_solution(6040083401829026422)
XLA Ops:
  0.0 0.9 copy-done.1
  0.9 0.8 copy-done.2
  1.8 0.5 collective-permute-start
  2.3 4.8 %collective-permute-done = bf16[256,256]{1,0:T(8,128)(2,1)S(1)} collective-permute-done((bf16[256,256]{1,0:T(8,128)(2,1)S(1)}, bf16[256,256]{1,0:T(8,128)(2,1)S(1)}, u32[]{:S(2)}, u32[]{:S(2)}) %collective-permute-start) | collective-permute-done | bytes 131104 | tf_op jit(solution)/shard_map/ppermute | solution.py:35
  7.1 0.6 collective-permute-start.6
  7.9 3.2 %collective-permute-start.4 = (bf16[256,256]{1,0:T(8,128)(2,1)S(1)}, bf16[256,256]{1,0:T(8,128)(2,1)S(1)}, u32[]{:S(2)}, u32[]{:S(2)}) collective-permute-start(bf16[256,256]{1,0:T(8,128)(2,1)S(1)} %pad_maximum_fusion.2), channel_id=1, source_target_pairs={{0,32},{1,9},{2,34},{3,11},{4,36},{5,13},{6,38},{7,15},{8,40},{9,1... | collective-permute-start | bytes 393224 | tf_op jit(solution)/shard_map/ppermute | solution.py:35
  11.1 1.5 collective-permute-start.3
  12.6 1.2 collective-permute-done.6.rest_5_
  13.8 2.0 %collective-permute-start.1 = (bf16[256,256]{1,0:T(8,128)(2,1)S(1)}, bf16[256,256]{1,0:T(8,128)(2,1)S(1)}, u32[]{:S(2)}, u32[]{:S(2)}) collective-permute-start(bf16[256,256]{1,0:T(8,128)(2,1)S(1)} %pad_maximum_fusion.1), channel_id=1, source_target_pairs={{0,8},{1,33},{2,10},{3,35},{4,12},{5,37},{6,14},{7,39},{8,16},{9,4... | collective-permute-start | bytes 393224 | tf_op jit(solution)/shard_map/ppermute | solution.py:35
  15.8 3.1 %attend_own.1 = (f32[8,256,128]{2,1,0:T(8,128)S(1)}, f32[8,256,256]{2,1,0:T(8,128)S(1)}) custom-call(s32[5]{0:T(128)S(1)} %stack.23.place, bf16[256,1024]{1,0:T(8,128)(2,1)S(1)} %copy-done, bf16[512,256]{1,0:T(8,128)(2,1)S(1)} %pad_maximum_fusion.own), custom_call_target="tpu_custom_call" | custom-call | flops 536870912 | bytes 8388608 | tf_op jit(solution)/shard_map/attend_own/pallas_call | solution.py:212
  19.2 3.2 %collective-permute-start.9 = (bf16[1024,256]{1,0:T(8,128)(2,1)S(1)}, bf16[1024,256]{1,0:T(8,128)(2,1)S(1)}, u32[]{:S(2)}, u32[]{:S(2)}) collective-permute-start(bf16[1024,256]{1,0:T(8,128)(2,1)S(1)} %constant_dynamic-update-slice_fusion.5), channel_id=1, source_target_pairs={{0,32},{1,9},{2,34},{3,11},{4,36},{5,13},{6,38},{7,15},{8,40},{9,1... | collective-permute-start | bytes 1572872 | tf_op jit(solution)/shard_map/ppermute | solution.py:35
  22.5 1.7 collective-permute-start.8
  24.1 1.6 collective-permute-start.7
  25.8 25.6 %attend_step.3 = (f32[8,256,128]{2,1,0:T(8,128)S(1)}, f32[8,256,256]{2,1,0:T(8,128)S(1)}) custom-call(s32[5]{0:T(128)S(1)} %stack.23.place, bf16[256,1024]{1,0:T(8,128)(2,1)S(1)} %copy-done, f32[8,256,128]{2,1,0:T(8,128)S(1)} %get-tuple-element.43.top_in, f32[8,256,256]{2,1,0:T(8,128)S(1)} %get-tuple-element.44.acc_in, ...), custom_call_target="tpu_custom_call" | custom-call | flops 2147483648 | bytes 8388608 | tf_op jit(solution)/shard_map/attend_step/pallas_call | solution.py:212
  51.4 6.5 %attend_step.4 = (f32[8,256,128]{2,1,0:T(8,128)S(1)}, f32[8,256,256]{2,1,0:T(8,128)S(1)}) custom-call(s32[5]{0:T(128)S(1)} %stack.23.place, bf16[256,1024]{1,0:T(8,128)(2,1)S(1)} %copy-done, f32[8,256,128]{2,1,0:T(8,128)S(1)} %get-tuple-element.47.top_in, f32[8,256,256]{2,1,0:T(8,128)S(1)} %get-tuple-element.48.acc_in, ...), custom_call_target="tpu_custom_call" | custom-call | flops 2147483648 | bytes 8388608 | tf_op jit(solution)/shard_map/attend_step/pallas_call | solution.py:212
  58.1 33.9 %attend_step.5 = (f32[8,256,128]{2,1,0:T(8,128)S(1)}, f32[8,256,256]{2,1,0:T(8,128)S(1)}) custom-call(s32[5]{0:T(128)S(1)} %stack.23.place, bf16[256,1024]{1,0:T(8,128)(2,1)S(1)} %copy-done, f32[8,256,128]{2,1,0:T(8,128)S(1)} %get-tuple-element.53.top_in, f32[8,256,256]{2,1,0:T(8,128)S(1)} %get-tuple-element.54.acc_in, ...), custom_call_target="tpu_custom_call" | custom-call | flops 2147483648 | bytes 8388608 | tf_op jit(solution)/shard_map/attend_step/pallas_call | solution.py:212
  92.1 35.6 %attend_last.1 = (bf16[256,1024]{1,0:T(8,128)(2,1)S(1)}, bf16[256,2048]{1,0:T(8,128)(2,1)S(1)}) custom-call(s32[5]{0:T(128)S(1)} %stack.23.place, bf16[256,1024]{1,0:T(8,128)(2,1)S(1)} %copy-done, f32[8,256,128]{2,1,0:T(8,128)S(1)} %get-tuple-element.57.top_in, f32[8,256,256]{2,1,0:T(8,128)S(1)} %get-tuple-element.58.acc_in, ...), custom_call_target="tpu_custom_call" | custom-call | flops 2147483648 | bytes 8388608 | tf_op jit(solution)/shard_map/attend_last/pallas_call | solution.py:212
  127.7 4.7 %collective-permute-start.13 = (bf16[256,2048]{1,0:T(8,128)(2,1)S(1)}, bf16[256,2048]{1,0:T(8,128)(2,1)S(1)}, u32[]{:S(2)}, u32[]{:S(2)}) collective-permute-start(bf16[256,2048]{1,0:T(8,128)(2,1)S(1)} %get-tuple-element.62), channel_id=1, source_target_pairs={{0,1},{1,0},{2,3},{3,2},{4,5},{5,4},{6,7},{7,6},{8,9},{9,8},{10,11... | collective-permute-start | bytes 3145736 | tf_op jit(solution)/shard_map/ppermute | solution.py:35
  132.3 3.0 %project.3 = bf16[256,2048]{1,0:T(8,128)(2,1)S(1)} custom-call(s32[1]{0:T(128)} %bitcast.6.part, bf16[256,1024]{1,0:T(8,128)(2,1)S(1)} %get-tuple-element.63.heads_ref, bf16[1024,8192]{1,0:T(8,128)(2,1)} %w_ref.5), custom_call_target="tpu_custom_call" | custom-call | flops 1073741824 | bytes 6291456 | tf_op jit(solution)/shard_map/project/pallas_call | solution.py:242
  135.8 3.0 %project.5 = bf16[256,2048]{1,0:T(8,128)(2,1)S(1)} custom-call(s32[1]{0:T(128)} %bitcast.7.part, bf16[256,1024]{1,0:T(8,128)(2,1)S(1)} %get-tuple-element.63.heads_ref, bf16[1024,8192]{1,0:T(8,128)(2,1)} %w_ref.5), custom_call_target="tpu_custom_call" | custom-call | flops 1073741824 | bytes 6291456 | tf_op jit(solution)/shard_map/project/pallas_call | solution.py:242
  138.9 2.4 %collective-permute-start.15 = (bf16[256,2048]{1,0:T(8,128)(2,1)S(1)}, bf16[256,2048]{1,0:T(8,128)(2,1)S(1)}, u32[]{:S(2)}, u32[]{:S(2)}) collective-permute-start(bf16[256,2048]{1,0:T(8,128)(2,1)S(1)} %add_convert_fusion.1), channel_id=1, source_target_pairs={{0,2},{1,3},{2,0},{3,1},{4,6},{5,7},{6,4},{7,5},{8,10},{9,11},{10,... | collective-permute-start | bytes 3145736 | tf_op jit(solution)/shard_map/ppermute | solution.py:35
  141.3 3.0 %project.4 = bf16[256,2048]{1,0:T(8,128)(2,1)S(1)} custom-call(s32[1]{0:T(128)} %bitcast.part, bf16[256,1024]{1,0:T(8,128)(2,1)S(1)} %get-tuple-element.63.heads_ref, bf16[1024,8192]{1,0:T(8,128)(2,1)} %w_ref.5), custom_call_target="tpu_custom_call" | custom-call | flops 1073741824 | bytes 6291456 | tf_op jit(solution)/shard_map/project/pallas_call | solution.py:242
  144.3 21.6 %collective-permute-done.15 = bf16[256,2048]{1,0:T(8,128)(2,1)S(1)} collective-permute-done((bf16[256,2048]{1,0:T(8,128)(2,1)S(1)}, bf16[256,2048]{1,0:T(8,128)(2,1)S(1)}, u32[]{:S(2)}, u32[]{:S(2)}) %collective-permute-start.15) | collective-permute-done | bytes 1048608 | tf_op jit(solution)/shard_map/ppermute | solution.py:35
  166.0 1.5 add_convert_fusion
  (36 shorter events, 1.0 us)
Async XLA Ops:
  0.0 15.8 %copy-start = (bf16[256,1024]{1,0:T(8,128)(2,1)S(1)}, bf16[256,1024]{1,0:T(8,128)(2,1)}, u32[]{:S(2)}) copy-start(bf16[256,1024]{1,0:T(8,128)(2,1)} %q_ref.9) | copy-start | bytes 1572868
  0.0 0.9 copy-start.1
  0.9 0.8 copy-start.2
  1.8 5.3 %collective-permute-start = (bf16[256,256]{1,0:T(8,128)(2,1)S(1)}, bf16[256,256]{1,0:T(8,128)(2,1)S(1)}, u32[]{:S(2)}, u32[]{:S(2)}) collective-permute-start(bf16[256,256]{1,0:T(8,128)(2,1)S(1)} %pack.1), channel_id=1, source_target_pairs={{0,4},{1,5},{2,6},{3,7},{4,0},{5,1},{6,2},{7,3},{8,12},{9,13},{10,... | collective-permute-start | bytes 393224 | tf_op jit(solution)/shard_map/ppermute | solution.py:35
  7.1 6.7 %collective-permute-start.6 = (bf16[256,256]{1,0:T(8,128)(2,1)S(1)}, bf16[256,256]{1,0:T(8,128)(2,1)S(1)}, u32[]{:S(2)}, u32[]{:S(2)}) collective-permute-start(bf16[256,256]{1,0:T(8,128)(2,1)S(1)} %pad_maximum_fusion.2), channel_id=1, source_target_pairs={{0,64},{1,17},{2,66},{3,19},{4,68},{5,21},{6,70},{7,23},{8,72},{9,... | collective-permute-start | bytes 393224 | tf_op jit(solution)/shard_map/ppermute | solution.py:35
  7.8 11.2 %collective-permute-start.5 = (bf16[256,256]{1,0:T(8,128)(2,1)S(1)}, bf16[256,256]{1,0:T(8,128)(2,1)S(1)}, u32[]{:S(2)}, u32[]{:S(2)}) collective-permute-start(bf16[256,256]{1,0:T(8,128)(2,1)S(1)} %pad_maximum_fusion.2), channel_id=1, source_target_pairs={{0,96},{1,25},{2,98},{3,27},{4,100},{5,29},{6,102},{7,31},{8,104},... | collective-permute-start | bytes 393224 | tf_op jit(solution)/shard_map/ppermute | solution.py:35
  7.9 11.2 %collective-permute-start.4 = (bf16[256,256]{1,0:T(8,128)(2,1)S(1)}, bf16[256,256]{1,0:T(8,128)(2,1)S(1)}, u32[]{:S(2)}, u32[]{:S(2)}) collective-permute-start(bf16[256,256]{1,0:T(8,128)(2,1)S(1)} %pad_maximum_fusion.2), channel_id=1, source_target_pairs={{0,32},{1,9},{2,34},{3,11},{4,36},{5,13},{6,38},{7,15},{8,40},{9,1... | collective-permute-start | bytes 393224 | tf_op jit(solution)/shard_map/ppermute | solution.py:35
  11.1 7.9 %collective-permute-start.3 = (bf16[256,256]{1,0:T(8,128)(2,1)S(1)}, bf16[256,256]{1,0:T(8,128)(2,1)S(1)}, u32[]{:S(2)}, u32[]{:S(2)}) collective-permute-start(bf16[256,256]{1,0:T(8,128)(2,1)S(1)} %pad_maximum_fusion.1), channel_id=1, source_target_pairs={{0,16},{1,65},{2,18},{3,67},{4,20},{5,69},{6,22},{7,71},{8,24},{9,... | collective-permute-start | bytes 393224 | tf_op jit(solution)/shard_map/ppermute | solution.py:35
  12.6 6.5 %collective-permute-start.2 = (bf16[256,256]{1,0:T(8,128)(2,1)S(1)}, bf16[256,256]{1,0:T(8,128)(2,1)S(1)}, u32[]{:S(2)}, u32[]{:S(2)}) collective-permute-start(bf16[256,256]{1,0:T(8,128)(2,1)S(1)} %pad_maximum_fusion.1), channel_id=1, source_target_pairs={{0,24},{1,97},{2,26},{3,99},{4,28},{5,101},{6,30},{7,103},{8,0},{9... | collective-permute-start | bytes 393224 | tf_op jit(solution)/shard_map/ppermute | solution.py:35
  13.8 5.3 %collective-permute-start.1 = (bf16[256,256]{1,0:T(8,128)(2,1)S(1)}, bf16[256,256]{1,0:T(8,128)(2,1)S(1)}, u32[]{:S(2)}, u32[]{:S(2)}) collective-permute-start(bf16[256,256]{1,0:T(8,128)(2,1)S(1)} %pad_maximum_fusion.1), channel_id=1, source_target_pairs={{0,8},{1,33},{2,10},{3,35},{4,12},{5,37},{6,14},{7,39},{8,16},{9,4... | collective-permute-start | bytes 393224 | tf_op jit(solution)/shard_map/ppermute | solution.py:35
  19.1 32.2 %collective-permute-start.10 = (bf16[1024,256]{1,0:T(8,128)(2,1)S(1)}, bf16[1024,256]{1,0:T(8,128)(2,1)S(1)}, u32[]{:S(2)}, u32[]{:S(2)}) collective-permute-start(bf16[1024,256]{1,0:T(8,128)(2,1)S(1)} %constant_dynamic-update-slice_fusion.5), channel_id=1, source_target_pairs={{0,96},{1,25},{2,98},{3,27},{4,100},{5,29},{6,102},{7,31},{8,104},... | collective-permute-start | bytes 1572872 | tf_op jit(solution)/shard_map/ppermute | solution.py:35
  19.2 32.1 %collective-permute-start.9 = (bf16[1024,256]{1,0:T(8,128)(2,1)S(1)}, bf16[1024,256]{1,0:T(8,128)(2,1)S(1)}, u32[]{:S(2)}, u32[]{:S(2)}) collective-permute-start(bf16[1024,256]{1,0:T(8,128)(2,1)S(1)} %constant_dynamic-update-slice_fusion.5), channel_id=1, source_target_pairs={{0,32},{1,9},{2,34},{3,11},{4,36},{5,13},{6,38},{7,15},{8,40},{9,1... | collective-permute-start | bytes 1572872 | tf_op jit(solution)/shard_map/ppermute | solution.py:35
  22.5 35.5 %collective-permute-start.8 = (bf16[1024,256]{1,0:T(8,128)(2,1)S(1)}, bf16[1024,256]{1,0:T(8,128)(2,1)S(1)}, u32[]{:S(2)}, u32[]{:S(2)}) collective-permute-start(bf16[1024,256]{1,0:T(8,128)(2,1)S(1)} %constant_dynamic-update-slice_fusion), channel_id=1, source_target_pairs={{0,24},{1,97},{2,26},{3,99},{4,28},{5,101},{6,30},{7,103},{8,0},{9... | collective-permute-start | bytes 1572872 | tf_op jit(solution)/shard_map/ppermute | solution.py:35
  24.1 33.9 %collective-permute-start.7 = (bf16[1024,256]{1,0:T(8,128)(2,1)S(1)}, bf16[1024,256]{1,0:T(8,128)(2,1)S(1)}, u32[]{:S(2)}, u32[]{:S(2)}) collective-permute-start(bf16[1024,256]{1,0:T(8,128)(2,1)S(1)} %constant_dynamic-update-slice_fusion), channel_id=1, source_target_pairs={{0,8},{1,33},{2,10},{3,35},{4,12},{5,37},{6,14},{7,39},{8,16},{9,4... | collective-permute-start | bytes 1572872 | tf_op jit(solution)/shard_map/ppermute | solution.py:35
  51.4 40.7 %collective-permute-start.11 = (bf16[1024,256]{1,0:T(8,128)(2,1)S(1)}, bf16[1024,256]{1,0:T(8,128)(2,1)S(1)}, u32[]{:S(2)}, u32[]{:S(2)}) collective-permute-start(bf16[1024,256]{1,0:T(8,128)(2,1)S(1)} %constant_dynamic-update-slice_fusion.5), channel_id=1, source_target_pairs={{0,64},{1,17},{2,66},{3,19},{4,68},{5,21},{6,70},{7,23},{8,72},{9,... | collective-permute-start | bytes 1572872 | tf_op jit(solution)/shard_map/ppermute | solution.py:35
  58.0 34.0 %collective-permute-start.12 = (bf16[1024,256]{1,0:T(8,128)(2,1)S(1)}, bf16[1024,256]{1,0:T(8,128)(2,1)S(1)}, u32[]{:S(2)}, u32[]{:S(2)}) collective-permute-start(bf16[1024,256]{1,0:T(8,128)(2,1)S(1)} %constant_dynamic-update-slice_fusion), channel_id=1, source_target_pairs={{0,16},{1,65},{2,18},{3,67},{4,20},{5,69},{6,22},{7,71},{8,24},{9,... | collective-permute-start | bytes 1572872 | tf_op jit(solution)/shard_map/ppermute | solution.py:35
  127.7 7.7 %collective-permute-start.13 = (bf16[256,2048]{1,0:T(8,128)(2,1)S(1)}, bf16[256,2048]{1,0:T(8,128)(2,1)S(1)}, u32[]{:S(2)}, u32[]{:S(2)}) collective-permute-start(bf16[256,2048]{1,0:T(8,128)(2,1)S(1)} %get-tuple-element.62), channel_id=1, source_target_pairs={{0,1},{1,0},{2,3},{3,2},{4,5},{5,4},{6,7},{7,6},{8,9},{9,8},{10,11... | collective-permute-start | bytes 3145736 | tf_op jit(solution)/shard_map/ppermute | solution.py:35
  138.8 5.5 %collective-permute-start.14 = (bf16[256,2048]{1,0:T(8,128)(2,1)S(1)}, bf16[256,2048]{1,0:T(8,128)(2,1)S(1)}, u32[]{:S(2)}, u32[]{:S(2)}) collective-permute-start(bf16[256,2048]{1,0:T(8,128)(2,1)S(1)} %project.5), channel_id=1, source_target_pairs={{0,1},{1,0},{2,3},{3,2},{4,5},{5,4},{6,7},{7,6},{8,9},{9,8},{10,11... | collective-permute-start | bytes 3145736 | tf_op jit(solution)/shard_map/ppermute | solution.py:35
  138.9 27.1 %collective-permute-start.15 = (bf16[256,2048]{1,0:T(8,128)(2,1)S(1)}, bf16[256,2048]{1,0:T(8,128)(2,1)S(1)}, u32[]{:S(2)}, u32[]{:S(2)}) collective-permute-start(bf16[256,2048]{1,0:T(8,128)(2,1)S(1)} %add_convert_fusion.1), channel_id=1, source_target_pairs={{0,2},{1,3},{2,0},{3,1},{4,6},{5,7},{6,4},{7,5},{8,10},{9,11},{10,... | collective-permute-start | bytes 3145736 | tf_op jit(solution)/shard_map/ppermute | solution.py:35

commit v2 on v1

--- a/solution.py
+++ b/solution.py
@@ -15,7 +15,7 @@
 LIMIT = 60.0
 
 STEPS = (1, 3, 2)
-BLK = 256
+BLK = 512
 
 
 def flat(z, x, y, h, c):
@@ -81,11 +81,9 @@
     rows = q_ref.shape[0]
     top[...] = jnp.full(top.shape, -1e30, jnp.float32)
     acc[...] = jnp.zeros(acc.shape, jnp.float32)
-    r = lax.broadcasted_iota(jnp.int32, (rows, 2 * BLK), 0)
-    k = lax.broadcasted_iota(jnp.int32, (rows, 2 * BLK), 1)
-    position = lax.div(k, 256) * 128 + lax.rem(k, 128)
-    position = position + jnp.where(lax.rem(lax.div(k, 128), 2) == 0, 0, jnp.where(y == 0, 256, -256))
-    valid = position <= r
+    r = lax.broadcasted_iota(jnp.int32, (rows, BLK), 0)
+    k = lax.broadcasted_iota(jnp.int32, (rows, BLK), 1)
+    valid = jnp.where(k < 256, k, k + jnp.where(y == 0, 0, -512)) <= r
 
     def head(h, carry):
         exact_fold(h, q_ref, own[...], valid, top, acc)
@@ -122,19 +120,15 @@
     top[...] = top_in[...]
     acc[...] = acc_in[...]
 
-    def keys_at(i, n):
-        return held[pl.ds(pl.multiple_of(i * n, n), n), :]
-
-    def odd(w):
-        return fast_fold(q_ref, keys_at(count - 1, BLK), top, acc, w)
+    def keys_at(i):
+        return held[pl.ds(pl.multiple_of(i * BLK, BLK), BLK), :]
 
     worst = lax.fori_loop(
         0,
-        lax.div(count, 2),
-        lambda i, w: fast_fold(q_ref, keys_at(i, 2 * BLK), top, acc, w),
+        count,
+        lambda i, w: fast_fold(q_ref, keys_at(i), top, acc, w),
         jnp.full((8, HD), -1e30, jnp.float32),
     )
-    worst = lax.cond(lax.rem(count, 2) == 1, odd, lambda w: w, worst)
 
     @pl.when(jnp.max(worst) > LIMIT)
     def _():
@@ -142,7 +136,7 @@
 
         def again(i, carry):
             def head(h, c):
-                exact_fold(h, q_ref, keys_at(i, BLK), None, top, acc)
+                exact_fold(h, q_ref, keys_at(i), None, top, acc)
                 return c
 
             return lax.fori_loop(0, acc.shape[0], head, carry)
@@ -189,7 +183,7 @@
 
 
 def cost(blocks, mib):
-    n = blocks * 512 * 2048
+    n = blocks * BLK * 2048
     return pl.CostEstimate(flops=4 * n * HD, bytes_accessed=mib << 20, transcendentals=n)
 
 
@@ -216,7 +210,7 @@
         out_specs=(VMEM, VMEM),
         scratch_shapes=held + (buffers + W_SCRATCH if last else []),
         compiler_params=pltpu.CompilerParams(vmem_limit_bytes=(45 if last else 20) << 20),
-        cost_estimate=cost(1 if first else 4, 8),
+        cost_estimate=cost(1 if first else sum(len(b) for b in blocks), 8),
         name="attend_last" if last else "attend_own" if first else "attend_step",
     )(place, queries, *in_state, *arrays, *([projection] if last else []))
 
@@ -262,31 +256,21 @@
 
     both = pack(key_rows, value_rows)
     near = send(both, lambda z, x, y, h, c: (z, x, y + 1, h, c))
-    pair_a = jnp.concatenate([both[:128], near[:128]], axis=0)
-    pair_b = jnp.concatenate([both[128:], near[128:]], axis=0)
-    own = jnp.concatenate([pair_a, pair_b], axis=0)
-    first_a = [along(pair_a, d, False) for d in STEPS]
-    first_b = [along(pair_b, d, True) for d in STEPS]
+    own = jnp.concatenate([both, near], axis=0)
+    first = [along(own, d, False) for d in STEPS]
     state = attend(place, queries, None, own, [])
-    first_a, first_b, state = lax.optimization_barrier((first_a, first_b, state))
-    all_a = jnp.concatenate([pair_a] + first_a, axis=0)
-    all_b = jnp.concatenate([pair_b] + first_b, axis=0)
-
-    def runs(d, a):
-        return [((4 - e) % 4, 4 - d) if a else (4 - d, (4 - e) % 4) for e in (0,) + STEPS]
-
-    near_a = [(along(all_a, d, True), runs(d, True)) for d in STEPS[:2]]
-    near_b = [(along(all_b, d, False), runs(d, False)) for d in STEPS[:2]]
-    early = [(a, [(4 - d, 0)]) for a, d in zip(first_a, STEPS)] + [(b, [(0, 4 - d)]) for b, d in zip(first_b, STEPS)]
-    state = attend(place, queries, state, None, early)
-    arrays, all_a, state = lax.optimization_barrier(([a for a, _ in near_a], all_a, state))
-    far_a = along(all_a, STEPS[2], True)
-    state = attend(place, queries, state, None, [(a, r) for a, (_, r) in zip(arrays, near_a)])
-    arrays, all_b, state = lax.optimization_barrier(([b for b, _ in near_b], all_b, state))
-    far_b = along(all_b, STEPS[2], False)
-    state = attend(place, queries, state, None, [(b, r) for b, (_, r) in zip(arrays, near_b)])
-    rest = [(far_a, runs(STEPS[2], True)), (far_b, runs(STEPS[2], False))]
-    heads_out, far = attend(place, queries, state, None, rest, projection)
+    first, state = lax.optimization_barrier((first, state))
+    line = jnp.concatenate([own] + first, axis=0)
+
+    def runs(d):
+        return [((4 - e) % 4, 4 - d) for e in (0,) + STEPS]
+
+    lines = [along(line, d, True) for d in STEPS[:2]]
+    state = attend(place, queries, state, None, [(a, [(4 - d, 0)]) for a, d in zip(first, STEPS)])
+    lines, line, state = lax.optimization_barrier((lines, line, state))
+    last = along(line, STEPS[2], True)
+    state = attend(place, queries, state, None, [(a, runs(d)) for a, d in zip(lines, STEPS)])
+    heads_out, far = attend(place, queries, state, None, [(last, runs(STEPS[2]))], projection)
 
     far = send(far, lambda z, x, y, h, c: (z, x, y, h, c + 1))
     cross = add(project(heads_out, projection, tp ^ 2), far)

time: 168 us -> 146 us (0.87)
  the two profiles are of different devices: /device:TPU:110 before, /device:TPU:126 now
where the time goes in v2:
time: 146 us
  Pallas kernels  91.8 us (63%)
  waiting for transfers between devices  39.1 us (27%)
  starting transfers between devices  9.66 us (7%)
  local copies, waits for them, and re-layouts  2.88 us (2%)
  other arithmetic  1.91 us (1%)
    pallas_call x4, Pallas kernels, attend(): pl.pallas_call(own_kernel if first else functools.partial(step_kernel, la...  82.7 us
    ppermute x10, waiting for transfers between devices, send(): return lax.ppermute(a, AXES, pairs)  39.1 us
    ppermute x10, starting transfers between devices, send(): return lax.ppermute(a, AXES, pairs)  9.66 us
    pallas_call x3, Pallas kernels, project(): pl.pallas_call(project_kernel, out_shape=jax.ShapeDtypeStruct((rows, WIDT...  9.07 us
  transfers between devices with their start and end apart: 10, of which 5 were waited for; matrix products, arithmetic and copies ran while one was open for 0% of the time, Pallas kernels for 43%

profile of v2, /device:TPU:126, one launch (start us, length us, event | category | flops | bytes accessed | tf_op | source)
XLA Modules:
  0.0 145.5 jit_solution(3431359609609103894)
XLA Ops:
  0.0 0.8 copy-done.2
  0.8 0.8 copy-done.3
  1.7 0.8 collective-permute-start
  2.6 4.4 %collective-permute-done = bf16[256,256]{1,0:T(8,128)(2,1)S(1)} collective-permute-done((bf16[256,256]{1,0:T(8,128)(2,1)S(1)}, bf16[256,256]{1,0:T(8,128)(2,1)S(1)}, u32[]{:S(2)}, u32[]{:S(2)}) %collective-permute-start) | collective-permute-done | bytes 131104 | tf_op jit(solution)/shard_map/ppermute | solution.py:35
  7.0 0.5 collective-permute-start.1
  7.6 1.5 %collective-permute-start.2 = (bf16[512,256]{1,0:T(8,128)(2,1)S(1)}, bf16[512,256]{1,0:T(8,128)(2,1)S(1)}, u32[]{:S(2)}, u32[]{:S(2)}) collective-permute-start(bf16[512,256]{1,0:T(8,128)(2,1)S(1)} %pad_maximum_fusion.own), channel_id=1, source_target_pairs={{0,24},{1,97},{2,26},{3,99},{4,28},{5,101},{6,30},{7,103},{8,0},{9... | collective-permute-start | bytes 786440 | tf_op jit(solution)/shard_map/ppermute | solution.py:35
  9.1 1.4 collective-permute-start.3
  10.6 1.0 copy-done
  11.6 3.0 %attend_own.1 = (f32[8,256,128]{2,1,0:T(8,128)S(1)}, f32[8,256,256]{2,1,0:T(8,128)S(1)}) custom-call(s32[5]{0:T(128)S(1)} %stack.23.place, bf16[256,1024]{1,0:T(8,128)(2,1)S(1)} %copy-done, bf16[512,256]{1,0:T(8,128)(2,1)S(1)} %pad_maximum_fusion.own), custom_call_target="tpu_custom_call" | custom-call | flops 536870912 | bytes 8388608 | tf_op jit(solution)/shard_map/attend_own/pallas_call | solution.py:206
  14.7 3.3 %collective-permute-done.2.rest_1_ = bf16[512,256]{1,0:T(8,128)(2,1)S(1)} collective-permute-done((bf16[512,256]{1,0:T(8,128)(2,1)S(1)}, bf16[512,256]{1,0:T(8,128)(2,1)S(1)}, u32[]{:S(2)}, u32[]{:S(2)}) %collective-permute-start.2) | collective-permute-done | bytes 262176 | tf_op jit(solution)/shard_map/ppermute | solution.py:35
  18.1 2.0 %collective-permute-start.5 = (bf16[2048,256]{1,0:T(8,128)(2,1)S(1)}, bf16[2048,256]{1,0:T(8,128)(2,1)S(1)}, u32[]{:S(2)}, u32[]{:S(2)}) collective-permute-start(bf16[2048,256]{1,0:T(8,128)(2,1)S(1)} %constant_dynamic-update-slice_fusion), channel_id=1, source_target_pairs={{0,96},{1,25},{2,98},{3,27},{4,100},{5,29},{6,102},{7,31},{8,104},... | collective-permute-start | bytes 3145736 | tf_op jit(solution)/shard_map/ppermute | solution.py:35
  20.2 5.1 %attend_step.2 = (f32[8,256,128]{2,1,0:T(8,128)S(1)}, f32[8,256,256]{2,1,0:T(8,128)S(1)}) custom-call(s32[5]{0:T(128)S(1)} %stack.23.place, bf16[256,1024]{1,0:T(8,128)(2,1)S(1)} %copy-done, f32[8,256,128]{2,1,0:T(8,128)S(1)} %get-tuple-element.30.top_in, f32[8,256,256]{2,1,0:T(8,128)S(1)} %get-tuple-element.31.acc_in, ...), custom_call_target="tpu_custom_call" | custom-call | flops 1610612736 | bytes 8388608 | tf_op jit(solution)/shard_map/attend_step/pallas_call | solution.py:206
  25.3 7.7 %collective-permute-done.4.rest_0_ = bf16[2048,256]{1,0:T(8,128)(2,1)S(1)} collective-permute-done((bf16[2048,256]{1,0:T(8,128)(2,1)S(1)}, bf16[2048,256]{1,0:T(8,128)(2,1)S(1)}, u32[]{:S(2)}, u32[]{:S(2)}) %collective-permute-start.4) | collective-permute-done | bytes 1048608 | tf_op jit(solution)/shard_map/ppermute | solution.py:35
  32.9 1.3 collective-permute-done.5.rest_1_
  34.2 1.2 collective-permute-start.6
  35.4 48.1 %attend_step.3 = (f32[8,256,128]{2,1,0:T(8,128)S(1)}, f32[8,256,256]{2,1,0:T(8,128)S(1)}) custom-call(s32[5]{0:T(128)S(1)} %stack.23.place, bf16[256,1024]{1,0:T(8,128)(2,1)S(1)} %copy-done, f32[8,256,128]{2,1,0:T(8,128)S(1)} %get-tuple-element.34.top_in, f32[8,256,256]{2,1,0:T(8,128)S(1)} %get-tuple-element.35.acc_in, ...), custom_call_target="tpu_custom_call" | custom-call | flops 4294967296 | bytes 8388608 | tf_op jit(solution)/shard_map/attend_step/pallas_call | solution.py:206
  83.5 26.5 %attend_last.1 = (bf16[256,1024]{1,0:T(8,128)(2,1)S(1)}, bf16[256,2048]{1,0:T(8,128)(2,1)S(1)}) custom-call(s32[5]{0:T(128)S(1)} %stack.23.place, bf16[256,1024]{1,0:T(8,128)(2,1)S(1)} %copy-done.1, f32[8,256,128]{2,1,0:T(8,128)S(1)} %get-tuple-element.38.top_in, f32[8,256,256]{2,1,0:T(8,128)S(1)} %get-tuple-element.39.acc_in, ...), custom_call_target="tpu_custom_call" | custom-call | flops 2147483648 | bytes 8388608 | tf_op jit(solution)/shard_map/attend_last/pallas_call | solution.py:206
  110.3 3.0 %project.3 = bf16[256,2048]{1,0:T(8,128)(2,1)S(1)} custom-call(s32[1]{0:T(128)} %bitcast.6.part, bf16[256,1024]{1,0:T(8,128)(2,1)S(1)} %get-tuple-element.43.heads_ref, bf16[1024,8192]{1,0:T(8,128)(2,1)} %w_ref.5), custom_call_target="tpu_custom_call" | custom-call | flops 1073741824 | bytes 6291456 | tf_op jit(solution)/shard_map/project/pallas_call | solution.py:236
  113.7 3.0 %project.5 = bf16[256,2048]{1,0:T(8,128)(2,1)S(1)} custom-call(s32[1]{0:T(128)} %bitcast.7.part, bf16[256,1024]{1,0:T(8,128)(2,1)S(1)} %get-tuple-element.43.heads_ref, bf16[1024,8192]{1,0:T(8,128)(2,1)} %w_ref.5), custom_call_target="tpu_custom_call" | custom-call | flops 1073741824 | bytes 6291456 | tf_op jit(solution)/shard_map/project/pallas_call | solution.py:236
  116.8 0.6 collective-permute-start.8
  117.3 1.2 collective-permute-start.9
  118.6 3.0 %project.4 = bf16[256,2048]{1,0:T(8,128)(2,1)S(1)} custom-call(s32[1]{0:T(128)} %bitcast.part, bf16[256,1024]{1,0:T(8,128)(2,1)S(1)} %get-tuple-element.43.heads_ref, bf16[1024,8192]{1,0:T(8,128)(2,1)} %w_ref.5), custom_call_target="tpu_custom_call" | custom-call | flops 1073741824 | bytes 6291456 | tf_op jit(solution)/shard_map/project/pallas_call | solution.py:236
  121.6 22.4 %collective-permute-done.9 = bf16[256,2048]{1,0:T(8,128)(2,1)S(1)} collective-permute-done((bf16[256,2048]{1,0:T(8,128)(2,1)S(1)}, bf16[256,2048]{1,0:T(8,128)(2,1)S(1)}, u32[]{:S(2)}, u32[]{:S(2)}) %collective-permute-start.9) | collective-permute-done | bytes 1048608 | tf_op jit(solution)/shard_map/ppermute | solution.py:35
  144.0 1.5 %add_convert_fusion = bf16[256,2048]{1,0:T(8,128)(2,1)} fusion(bf16[256,2048]{1,0:T(8,128)(2,1)S(1)} %collective-permute-done.9, bf16[256,2048]{1,0:T(8,128)(2,1)S(1)} %collective-permute-done.8, bf16[256,2048]{1,0:T(8,128)(2,1)S(1)} %project.4), kind=kLoop, calls=%fused_computation | loop fusion | flops 3145728 | bytes 4194304 | tf_op jit(solution)/shard_map/convert_element_type | solution.py:283
  (21 shorter events, 1.0 us)
Async XLA Ops:
  0.0 0.8 copy-start.2
  0.8 0.8 copy-start.3
  1.7 5.3 %collective-permute-start = (bf16[256,256]{1,0:T(8,128)(2,1)S(1)}, bf16[256,256]{1,0:T(8,128)(2,1)S(1)}, u32[]{:S(2)}, u32[]{:S(2)}) collective-permute-start(bf16[256,256]{1,0:T(8,128)(2,1)S(1)} %pack.1), channel_id=1, source_target_pairs={{0,4},{1,5},{2,6},{3,7},{4,0},{5,1},{6,2},{7,3},{8,12},{9,13},{10,... | collective-permute-start | bytes 393224 | tf_op jit(solution)/shard_map/ppermute | solution.py:35
  7.0 7.6 %collective-permute-start.1 = (bf16[512,256]{1,0:T(8,128)(2,1)S(1)}, bf16[512,256]{1,0:T(8,128)(2,1)S(1)}, u32[]{:S(2)}, u32[]{:S(2)}) collective-permute-start(bf16[512,256]{1,0:T(8,128)(2,1)S(1)} %pad_maximum_fusion.own), channel_id=1, source_target_pairs={{0,8},{1,33},{2,10},{3,35},{4,12},{5,37},{6,14},{7,39},{8,16},{9,4... | collective-permute-start | bytes 786440 | tf_op jit(solution)/shard_map/ppermute | solution.py:35
  7.6 10.4 %collective-permute-start.2 = (bf16[512,256]{1,0:T(8,128)(2,1)S(1)}, bf16[512,256]{1,0:T(8,128)(2,1)S(1)}, u32[]{:S(2)}, u32[]{:S(2)}) collective-permute-start(bf16[512,256]{1,0:T(8,128)(2,1)S(1)} %pad_maximum_fusion.own), channel_id=1, source_target_pairs={{0,24},{1,97},{2,26},{3,99},{4,28},{5,101},{6,30},{7,103},{8,0},{9... | collective-permute-start | bytes 786440 | tf_op jit(solution)/shard_map/ppermute | solution.py:35
  9.1 8.8 %collective-permute-start.3 = (bf16[512,256]{1,0:T(8,128)(2,1)S(1)}, bf16[512,256]{1,0:T(8,128)(2,1)S(1)}, u32[]{:S(2)}, u32[]{:S(2)}) collective-permute-start(bf16[512,256]{1,0:T(8,128)(2,1)S(1)} %pad_maximum_fusion.own), channel_id=1, source_target_pairs={{0,16},{1,65},{2,18},{3,67},{4,20},{5,69},{6,22},{7,71},{8,24},{9,... | collective-permute-start | bytes 786440 | tf_op jit(solution)/shard_map/ppermute | solution.py:35
  10.6 1.0 copy-start
  18.1 14.9 %collective-permute-start.4 = (bf16[2048,256]{1,0:T(8,128)(2,1)S(1)}, bf16[2048,256]{1,0:T(8,128)(2,1)S(1)}, u32[]{:S(2)}, u32[]{:S(2)}) collective-permute-start(bf16[2048,256]{1,0:T(8,128)(2,1)S(1)} %constant_dynamic-update-slice_fusion), channel_id=1, source_target_pairs={{0,32},{1,9},{2,34},{3,11},{4,36},{5,13},{6,38},{7,15},{8,40},{9,1... | collective-permute-start | bytes 3145736 | tf_op jit(solution)/shard_map/ppermute | solution.py:35
  18.1 16.1 %collective-permute-start.5 = (bf16[2048,256]{1,0:T(8,128)(2,1)S(1)}, bf16[2048,256]{1,0:T(8,128)(2,1)S(1)}, u32[]{:S(2)}, u32[]{:S(2)}) collective-permute-start(bf16[2048,256]{1,0:T(8,128)(2,1)S(1)} %constant_dynamic-update-slice_fusion), channel_id=1, source_target_pairs={{0,96},{1,25},{2,98},{3,27},{4,100},{5,29},{6,102},{7,31},{8,104},... | collective-permute-start | bytes 3145736 | tf_op jit(solution)/shard_map/ppermute | solution.py:35
  34.2 49.3 %copy-start.1 = (bf16[256,1024]{1,0:T(8,128)(2,1)S(1)}, bf16[256,1024]{1,0:T(8,128)(2,1)}, u32[]{:S(2)}) copy-start(bf16[256,1024]{1,0:T(8,128)(2,1)} %q_ref.7) | copy-start | bytes 1572868
  34.2 49.3 %collective-permute-start.6 = (bf16[2048,256]{1,0:T(8,128)(2,1)S(1)}, bf16[2048,256]{1,0:T(8,128)(2,1)S(1)}, u32[]{:S(2)}, u32[]{:S(2)}) collective-permute-start(bf16[2048,256]{1,0:T(8,128)(2,1)S(1)} %constant_dynamic-update-slice_fusion), channel_id=1, source_target_pairs={{0,64},{1,17},{2,66},{3,19},{4,68},{5,21},{6,70},{7,23},{8,72},{9,... | collective-permute-start | bytes 3145736 | tf_op jit(solution)/shard_map/ppermute | solution.py:35
  110.0 3.3 %collective-permute-start.7 = (bf16[256,2048]{1,0:T(8,128)(2,1)S(1)}, bf16[256,2048]{1,0:T(8,128)(2,1)S(1)}, u32[]{:S(2)}, u32[]{:S(2)}) collective-permute-start(bf16[256,2048]{1,0:T(8,128)(2,1)S(1)} %get-tuple-element.42), channel_id=1, source_target_pairs={{0,1},{1,0},{2,3},{3,2},{4,5},{5,4},{6,7},{7,6},{8,9},{9,8},{10,11... | collective-permute-start | bytes 3145736 | tf_op jit(solution)/shard_map/ppermute | solution.py:35
  116.8 4.8 %collective-permute-start.8 = (bf16[256,2048]{1,0:T(8,128)(2,1)S(1)}, bf16[256,2048]{1,0:T(8,128)(2,1)S(1)}, u32[]{:S(2)}, u32[]{:S(2)}) collective-permute-start(bf16[256,2048]{1,0:T(8,128)(2,1)S(1)} %project.5), channel_id=1, source_target_pairs={{0,1},{1,0},{2,3},{3,2},{4,5},{5,4},{6,7},{7,6},{8,9},{9,8},{10,11... | collective-permute-start | bytes 3145736 | tf_op jit(solution)/shard_map/ppermute | solution.py:35
  117.3 26.7 %collective-permute-start.9 = (bf16[256,2048]{1,0:T(8,128)(2,1)S(1)}, bf16[256,2048]{1,0:T(8,128)(2,1)S(1)}, u32[]{:S(2)}, u32[]{:S(2)}) collective-permute-start(bf16[256,2048]{1,0:T(8,128)(2,1)S(1)} %add_convert_fusion.1), channel_id=1, source_target_pairs={{0,2},{1,3},{2,0},{3,1},{4,6},{5,7},{6,4},{7,5},{8,10},{9,11},{10,... | collective-permute-start | bytes 3145736 | tf_op jit(solution)/shard_map/ppermute | solution.py:35
